TPU v7x, 32 devices: a whole 2x2x4 slice. The times are simulated.
32 devices in a mesh: groups: 2 (over y), pts: 4 (over z), cb: 4 (over x, core).
Axes of the slice: x: 2, y: 2, z: 4, core: 2. Of those that a mesh axis runs over, the one named last changes fastest.
Arguments:
- points: bfloat16 [16384, 768], P(('groups', 'pts')), parts along dimension 0, may hold values from -60 to 60
- code_one: int32 [16384], P(('groups', 'pts')), parts along dimension 0, may hold values from 0 to 2047
- code_two: int32 [16384], P(('groups', 'pts')), parts along dimension 0, may hold values from 0 to 2047
- cent_one: bfloat16 [4096, 768], P(('groups', 'cb')), parts along dimension 0, may hold values from -6 to 6
- cent_two: bfloat16 [4096, 768], P(('groups', 'cb')), parts along dimension 0, may hold values from -6 to 6
Outputs:
- new_one: bfloat16 [4096, 768], P(('groups', 'cb')), parts along dimension 0
- new_two: bfloat16 [4096, 768], P(('groups', 'cb')), parts along dimension 0
- distortion: float32 [4], P('groups'), parts along dimension 0
There are 2 independent parts, one for each index of `groups`. A program takes and returns all parts, laid end to end along the dimension named above; each array names one. Nothing has to cross between parts.
All inputs are finite; a program needn't handle non-finite values.
Results may differ from a plain program's by a relative error of at most 0.0014.
Values may be sent and summed in bfloat16 or wider, within the bound.
A program may use at most 64 MiB of HBM per device.

v0:
```python
import jax
import jax.numpy as jnp
from jax import lax
from jax.sharding import PartitionSpec as P


def nearest_local(data, cents):
    sq = jnp.sum(jnp.square(data.astype(jnp.float32)), axis=1)
    csq = jnp.sum(jnp.square(cents.astype(jnp.float32)), axis=1)
    cross = lax.dot_general(
        data, cents, (((1,), (1,)), ((), ())), preferred_element_type=jnp.float32
    )
    dist = sq[:, None] - 2.0 * cross + csq[None, :]
    local_min = jnp.min(dist, axis=1)
    best = lax.pmin(local_min, "cb")
    return jnp.sum(best)


def section_update(data, codes, cents):
    rows = cents.shape[0]
    first = lax.axis_index("cb") * rows
    labels = first + lax.broadcasted_iota(jnp.int32, (1, rows), 1)
    onehot = (codes[:, None] == labels).astype(jnp.bfloat16)
    sums = lax.dot_general(
        onehot, data, (((0,), (0,)), ((), ())), preferred_element_type=jnp.float32
    )
    counts = jnp.sum(onehot.astype(jnp.float32), axis=0)
    share_sums, share_counts = (
        lax.psum_scatter(sums, "pts", scatter_dimension=0, tiled=True),
        lax.psum_scatter(counts, "pts", scatter_dimension=0, tiled=True),
    )
    share_rows = share_sums.shape[0]
    old_rows = lax.dynamic_slice_in_dim(cents, lax.axis_index("pts") * share_rows, share_rows, 0)
    return ((share_sums + old_rows.astype(jnp.float32)) / (share_counts + 1.0)[:, None]).astype(
        jnp.bfloat16
    )


def section_total(value):
    return lax.psum(value, "pts")


def local(points, code_one, code_two, cent_one, cent_two):
    rows = cent_one.shape[0]
    width = points.shape[1]
    npts = lax.axis_size("pts")
    ncb = lax.axis_size("cb")
    first = lax.axis_index("cb") * rows
    first_local = nearest_local(points, cent_one)
    updated_one = section_update(points, code_one, cent_one)
    gathered = lax.all_gather(updated_one, ("pts", "cb"), axis=0, tiled=True)
    share_rows = updated_one.shape[0]
    codebook = jnp.swapaxes(gathered.reshape(npts, ncb, share_rows, width), 0, 1).reshape(
        rows * ncb, width
    )
    new_one = lax.dynamic_slice_in_dim(codebook, first, rows, 0)
    looked = jnp.take(codebook, code_one, axis=0)
    residual = (points.astype(jnp.float32) - looked.astype(jnp.float32)).astype(jnp.bfloat16)
    updated_two = section_update(residual, code_two, cent_two)
    new_two = lax.all_gather(updated_two, "pts", axis=0, tiled=True)
    second_local = nearest_local(residual, cent_two)
    first_sum = section_total(first_local)
    second_sum = section_total(second_local)
    scale = jnp.float32(points.shape[0] * npts * width)
    distortion = jnp.stack([first_sum, second_sum]) / scale
    return (new_one, new_two, distortion)


def solution(mesh):
    return jax.shard_map(
        local,
        mesh=mesh,
        in_specs=(
            P(("groups", "pts"), None),
            P(("groups", "pts")),
            P(("groups", "pts")),
            P(("groups", "cb"), None),
            P(("groups", "cb"), None),
        ),
        out_specs=(P(("groups", "cb"), None), P(("groups", "cb"), None), P("groups")),
        check_vma=False,
    )
```

profile of v0, /device:TPU:0, one launch (start us, length us, event | category | flops | bytes accessed | tf_op | source)
XLA Modules:
  0.0 180.3 jit_solution(905735486691300784)
XLA Ops:
  7.3 5.2 %fusion.4 = f32[512,768]{1,0:T(8,128)} fusion(bf16[2048,768]{1,0:T(8,128)(2,1)} %param.5, s32[512]{0:T(512)S(1)} %iota_add_fusion, s32[2048]{0:T(1024)} %param.6), kind=kOutput, calls=%fused_computation.10 | convolution fusion | flops 1611661312 | bytes 4728832 | tf_op jit(solution)/shard_map/dot_general | solution.py:24
  13.8 1.2 convert_reduce_fusion
  15.1 13.9 %all-reduce = f32[512]{0:T(512)S(1)} all-reduce(f32[512]{0:T(512)S(1)} %get-tuple-element.4), channel_id=3, replica_groups=mesh['groups'=2,'pts'=4,'cb'=4] {'pts'}, use_global_device_ids=true, to_apply=%region_2.0.clone | all-reduce | flops 512 | bytes 4096
  29.0 21.9 %reduce-scatter.3.cloned.1.call-done = f32[128,768]{1,0:T(8,128)} async-done(((f32[512,768]{1,0:T(8,128)}), f32[128,768]{1,0:T(8,128)}) %reduce-scatter.3.cloned.1.call-update) | async-done | bytes 393232 | tf_op jit(solution)/shard_map/reduce_scatter | solution.py:29
  50.9 1.8 %divide_convert_fusion.1 = bf16[128,768]{1,0:T(8,128)(2,1)} fusion(f32[128,768]{1,0:T(8,128)} %reduce-scatter.3.cloned.1.call-done, f32[128]{0:T(128)S(1)} %dynamic-slice_add_fusion.1, bf16[512,768]{1,0:T(8,128)(2,1)} %param.8, s32[]{:T(128)S(6)} %select_n.16), kind=kLoop, calls=%fused_computation.23 | loop fusion | flops 393216 | bytes 786948 | tf_op jit(solution)/shard_map/convert_element_type | solution.py:34
  52.8 45.4 %all-gather.2.cloned.1.call-done = bf16[2048,768]{1,0:T(8,128)(2,1)} async-done(((bf16[128,768]{1,0:T(8,128)(2,1)}), bf16[2048,768]{1,0:T(8,128)(2,1)}) %all-gather.2.cloned.1.call-update) | async-done | bytes 3145744 | tf_op jit(solution)/shard_map/all_gather | solution.py:51
  98.2 2.1 %copy.10 = bf16[4,4,128,768]{3,2,1,0:T(8,128)(2,1)S(1)} copy(bf16[4,4,128,768]{3,2,0,1:T(8,128)(2,1)} %bitcast.15) | data formatting | bytes 6291456 | tf_op jit(solution)/shard_map/transpose | solution.py:53
  100.3 9.4 %gather_fusion = bf16[2048,768]{1,0:T(8,128)(2,1)} fusion(bf16[2048,768]{1,0:T(8,128)(2,1)S(1)} %bitcast.13, s32[2048]{0:T(1024)S(1)} %fusion.10), kind=kCustom, calls=%fused_computation | custom fusion | bytes 6299648 | tf_op jit(solution)/shard_map/jit(_take)/gather | solution.py:57
  109.7 4.3 %multiply_reduce_fusion = (f32[2048]{0:T(1024)S(1)}, bf16[2048,768]{1,0:T(8,128)(2,1)S(1)}, f32[2048]{0:T(1024)S(1)}) fusion(bf16[2048,768]{1,0:T(8,128)(2,1)} %gather_fusion, pred[2048]{0:T(1024)(128)(4,1)S(1)} %compare_and_fusion, bf16[2048,768]{1,0:T(8,128)(2,1)} %param.5), kind=kLoop, calls=%fused_computation.5 | loop fusion | flops 15724544 | bytes 9455616 | tf_op jit(solution)/shard_map/reduce_sum | solution.py:8
  114.0 1.7 copy-done.1
  115.7 3.3 %fusion.2 = f32[512,768]{1,0:T(8,128)} fusion(bf16[2048,768]{1,0:T(8,128)(2,1)S(1)} %get-tuple-element.11, s32[512]{0:T(512)S(1)} %iota_add_fusion, s32[2048]{0:T(1024)S(1)} %copy-done.4), kind=kOutput, calls=%fused_computation.7 | convolution fusion | flops 1611661312 | bytes 4728832 | tf_op jit(solution)/shard_map/dot_general | solution.py:24
  119.0 1.4 multiply_reduce_fusion.2
  120.4 1.4 multiply_reduce_fusion.1
  121.8 4.3 %add_reduce_fusion = f32[2048]{0:T(1024)S(1)} fusion(bf16[2048,768]{1,0:T(8,128)(2,1)} %copy-done.1, bf16[512,768]{1,0:T(8,128)(2,1)} %param.9, f32[512]{0:T(512)S(1)} %multiply_reduce_fusion.1, f32[2048]{0:T(1024)S(1)} %get-tuple-element.10), kind=kOutput, calls=%fused_computation.12 | convolution fusion | flops 1614804992 | bytes 3950592 | tf_op jit(solution)/shard_map/dot_general | solution.py:10
  126.2 1.8 %add_reduce_fusion.1 = f32[2048]{0:T(1024)S(1)} fusion(bf16[2048,768]{1,0:T(8,128)(2,1)S(1)} %copy-done, bf16[512,768]{1,0:T(8,128)(2,1)S(1)} %copy-done.2, f32[512]{0:T(512)S(1)} %multiply_reduce_fusion.2, f32[2048]{0:T(1024)S(1)} %get-tuple-element.12), kind=kOutput, calls=%fused_computation.13 | convolution fusion | flops 1614804992 | bytes 3950592 | tf_op jit(solution)/shard_map/dot_general | solution.py:10
  128.0 11.0 %all-reduce.3 = (f32[2048]{0:T(1024)S(1)}, f32[2048]{0:T(1024)S(1)}) all-reduce(f32[2048]{0:T(1024)S(1)} %add_reduce_fusion, f32[2048]{0:T(1024)S(1)} %add_reduce_fusion.1), channel_id=1, replica_groups=mesh['groups'=2,'pts'=4,'cb'=4] {'cb'}, use_global_device_ids=true, to_apply=%region_15.16 | all-reduce | flops 4096 | bytes 32768 | tf_op jit(solution)/shard_map/pmin | solution.py:15
  139.0 0.6 reduce_sum.79
  139.6 0.6 reduce_sum.76
  140.2 11.1 %all-reduce.2 = (f32[512]{0:T(512)S(1)}, f32[1]{0:T(128)}, f32[1]{0:T(128)}) all-reduce(f32[512]{0:T(512)S(1)} %get-tuple-element.3, f32[1]{0:T(128)} %bitcast.4, f32[1]{0:T(128)} %bitcast.3), channel_id=5, replica_groups=mesh['groups'=2,'pts'=4,'cb'=4] {'pts'}, use_global_device_ids=true, to_apply=%region_5.0.clone | all-reduce | flops 514 | bytes 4112
  151.4 1.9 %maximum_multiply_fusion = f32[2]{0:T(128)} fusion(f32[1]{0:T(128)} %get-tuple-element.6, f32[1]{0:T(128)} %get-tuple-element.7), kind=kLoop, calls=%fused_computation.29 | loop fusion | flops 4 | bytes 16 | tf_op jit(solution)/shard_map/div | solution.py:65
  153.2 0.9 constant_dynamic-slice_fusion
  154.2 1.1 divide_convert_fusion
  155.3 17.6 %all_gather.7 = bf16[512,768]{1,0:T(8,128)(2,1)S(1)} all-gather(bf16[128,768]{1,0:T(8,128)(2,1)S(1)} %divide_convert_fusion), channel_id=1, replica_groups=mesh['groups'=2,'pts'=4,'cb'=4] {'pts'}, dimensions={0}, use_global_device_ids=true | all-gather | bytes 983040 | tf_op jit(solution)/shard_map/all_gather | solution.py:60
  172.9 0.9 copy.12
  (24 shorter events, 1.0 us)
Async XLA Ops:
  7.2 43.7 %reduce-scatter.3.cloned.1.call-start = ((), (), s32[]{:S(2)}) async-start(), calls=%async_computation.2 | async-start | bytes 1966080 | tf_op jit(solution)/shard_map/reduce_scatter | solution.py:29
  7.2 5.3 %copy-start.5 = (u32[32]{0:T(128)S(1)}, u32[32]{0:T(128)}, u32[]{:S(2)}) copy-start(u32[32]{0:T(128)} %constant.42) | copy-start | bytes 388
  7.2 6.6 %copy-start.3 = (s32[2048]{0:T(1024)S(1)}, s32[2048]{0:T(1024)}, u32[]{:S(2)}) copy-start(s32[2048]{0:T(1024)} %param.6) | copy-start | bytes 24580
  7.3 6.6 %copy-start.4 = (s32[2048]{0:T(1024)S(1)}, s32[2048]{0:T(1024)}, u32[]{:S(2)}) copy-start(s32[2048]{0:T(1024)} %param.7) | copy-start | bytes 24580
  12.5 85.7 %all-gather.2.cloned.1.call-start = ((), (), s32[]{:S(2)}) async-start(), calls=%async_computation.3 | async-start | bytes 3342336 | tf_op jit(solution)/shard_map/all_gather | solution.py:51
  52.8 101.4 %reduce-scatter.5.cloned.1.call-start = ((), (), s32[]{:S(2)}) async-start(), calls=%async_computation.4 | async-start | bytes 1966080 | tf_op jit(solution)/shard_map/reduce_scatter | solution.py:29
  114.0 1.7 copy-start.1
  121.8 4.4 %copy-start = (bf16[2048,768]{1,0:T(8,128)(2,1)S(1)}, bf16[2048,768]{1,0:T(8,128)(2,1)}, u32[]{:S(2)}) copy-start(bf16[2048,768]{1,0:T(8,128)(2,1)} %param.5) | copy-start | bytes 9437188
  121.8 4.4 %copy-start.2 = (bf16[512,768]{1,0:T(8,128)(2,1)S(1)}, bf16[512,768]{1,0:T(8,128)(2,1)}, u32[]{:S(2)}) copy-start(bf16[512,768]{1,0:T(8,128)(2,1)} %param.8) | copy-start | bytes 2359300
Sparse Core Ops, SparseCore 0:
  12.6 38.2 reduce-scatter.2
  53.8 44.3 all-gather.1
  119.2 34.0 reduce-scatter.4
where the time goes:
time: 181 us; the launch traced here: 180 us
  waiting for transfers between devices  67.3 us (37%)
  blocking collectives  53.6 us (30%)
  local copies, waits for them, and re-layouts  15.6 us (9%)
  matrix products  14.7 us (8%)
  between operations  14.6 us (8%)
  other arithmetic  14.5 us (8%)
    all_gather x1, waiting for transfers between devices, local(): gathered = lax.all_gather(updated_one, ('pts', 'cb'), axis=0, tiled=True)  45.4 us
    unnamed x2, blocking collectives  25 us
    reduce_scatter x2, waiting for transfers between devices, section_update(): lax.psum_scatter(sums, 'pts', scatter_dimension=0, tiled=True)  21.9 us
    all_gather x1, blocking collectives, local(): new_two = lax.all_gather(updated_two, 'pts', axis=0, tiled=True)  17.6 us
    pmin x1, blocking collectives, nearest_local(): best = lax.pmin(local_min, 'cb')  11 us
    gather x1, local copies, waits for them, and re-layouts, local(): looked = jnp.take(codebook, code_one, axis=0)  9.38 us
    dot_general x2, matrix products, section_update(): lax.dot_general(onehot, data, (((0,), (0,)), ((), ())), preferred_element...  8.51 us
    dot_general x2, matrix products, nearest_local(): lax.dot_general(data, cents, (((1,), (1,)), ((), ())), preferred_element_...  6.18 us
  transfers between devices with their start and end apart: 3, of which 2 were waited for; matrix products, arithmetic and copies ran while one was open for 8% of the time, Pallas kernels for 0%

commit v1 on v0

--- a/solution.py
+++ b/solution.py
@@ -2,6 +2,16 @@
 import jax.numpy as jnp
 from jax import lax
 from jax.sharding import PartitionSpec as P
+
+
+def gather_by_hops(x, axis, d):
+    size = lax.axis_size(axis)
+    held, blocks = (x, [x])
+    for _ in range(size - 1):
+        held = lax.ppermute(held, axis, [(i, (i + 1) % size) for i in range(size)])
+        blocks.insert(0, held)
+    line = jnp.concatenate(blocks, axis=d)
+    return jnp.roll(line, (lax.axis_index(axis) + 1) * x.shape[d], axis=d)
 
 
 def nearest_local(data, cents):
@@ -57,7 +67,7 @@
     looked = jnp.take(codebook, code_one, axis=0)
     residual = (points.astype(jnp.float32) - looked.astype(jnp.float32)).astype(jnp.bfloat16)
     updated_two = section_update(residual, code_two, cent_two)
-    new_two = lax.all_gather(updated_two, "pts", axis=0, tiled=True)
+    new_two = gather_by_hops(updated_two, "pts", 0)
     second_local = nearest_local(residual, cent_two)
     first_sum = section_total(first_local)
     second_sum = section_total(second_local)

time: 181 us -> 188 us (1.039)
  waiting for transfers between devices: 67.3 us -> 89.5 us
  blocking collectives: 53.6 us -> 36 us
  local copies, waits for them, and re-layouts: 15.6 us -> 17.6 us
    ppermute x0 -> x3, waiting for transfers between devices: none -> 20.3 us  [gather_by_hops(): held = lax.ppermute(held, axis, [(i, (i + 1) % size) for i in range(size)])]
    all_gather x1 -> x0, blocking collectives: 17.6 us -> none  [local(): new_two = lax.all_gather(updated_two, 'pts', axis=0, tiled=True)]
    reduce_scatter x2, waiting for transfers between devices: 21.9 us -> 23.8 us  [section_update(): lax.psum_scatter(sums, 'pts', scatter_dimension=0, tiled=True)]
    unnamed x14 -> x20, local copies, waits for them, and re-layouts: 3.15 us -> 4.23 us
  transfers between devices with their start and end apart: 3 -> 6, of which waited for: 2 -> 6; matrix products, arithmetic and copies ran while one was open for 8% -> 8% of each run, Pallas kernels for 0% -> 0%
where the time goes in v1:
time: 188 us; the launch traced here: 187 us
  waiting for transfers between devices  89.5 us (48%)
  blocking collectives  36 us (19%)
  local copies, waits for them, and re-layouts  17.6 us (9%)
  matrix products  14.7 us (8%)
  between operations  14.6 us (8%)
  other arithmetic  14.5 us (8%)
    all_gather x1, waiting for transfers between devices, local(): gathered = lax.all_gather(updated_one, ('pts', 'cb'), axis=0, tiled=True)  45.4 us
    unnamed x2, blocking collectives  25 us
    reduce_scatter x2, waiting for transfers between devices, section_update(): lax.psum_scatter(sums, 'pts', scatter_dimension=0, tiled=True)  23.8 us
    ppermute x3, waiting for transfers between devices, gather_by_hops(): held = lax.ppermute(held, axis, [(i, (i + 1) % size) for i in range(size)])  20.3 us
    pmin x1, blocking collectives, nearest_local(): best = lax.pmin(local_min, 'cb')  11 us
    gather x1, local copies, waits for them, and re-layouts, local(): looked = jnp.take(codebook, code_one, axis=0)  9.38 us
    dot_general x2, matrix products, section_update(): lax.dot_general(onehot, data, (((0,), (0,)), ((), ())), preferred_element...  8.51 us
    dot_general x2, matrix products, nearest_local(): lax.dot_general(data, cents, (((1,), (1,)), ((), ())), preferred_element_...  6.18 us
  transfers between devices with their start and end apart: 6, of which 6 were waited for; matrix products, arithmetic and copies ran while one was open for 8% of the time, Pallas kernels for 0%

profile of v1, /device:TPU:0, one launch (start us, length us, event | category | flops | bytes accessed | tf_op | source)
XLA Modules:
  0.0 187.2 jit_solution(13931171131554714444)
XLA Ops:
  7.3 5.2 %fusion.4 = f32[512,768]{1,0:T(8,128)} fusion(bf16[2048,768]{1,0:T(8,128)(2,1)} %param.5, s32[512]{0:T(512)S(1)} %iota_add_fusion, s32[2048]{0:T(1024)} %param.6), kind=kOutput, calls=%fused_computation.10 | convolution fusion | flops 1611661312 | bytes 4728832 | tf_op jit(solution)/shard_map/dot_general | solution.py:34
  13.8 1.2 convert_reduce_fusion
  15.1 13.9 %all-reduce = f32[512]{0:T(512)S(1)} all-reduce(f32[512]{0:T(512)S(1)} %get-tuple-element.4), channel_id=3, replica_groups=mesh['groups'=2,'pts'=4,'cb'=4] {'pts'}, use_global_device_ids=true, to_apply=%region_2.0.clone | all-reduce | flops 512 | bytes 4096
  29.0 21.9 %reduce-scatter.3.cloned.1.call-done = f32[128,768]{1,0:T(8,128)} async-done(((f32[512,768]{1,0:T(8,128)}), f32[128,768]{1,0:T(8,128)}) %reduce-scatter.3.cloned.1.call-update) | async-done | bytes 393232 | tf_op jit(solution)/shard_map/reduce_scatter | solution.py:39
  50.9 1.8 divide_convert_fusion.1
  52.8 45.4 %all-gather.2.cloned.1.call-done = bf16[2048,768]{1,0:T(8,128)(2,1)} async-done(((bf16[128,768]{1,0:T(8,128)(2,1)}), bf16[2048,768]{1,0:T(8,128)(2,1)}) %all-gather.2.cloned.1.call-update) | async-done | bytes 3145744 | tf_op jit(solution)/shard_map/all_gather | solution.py:61
  98.2 2.1 %copy.10 = bf16[4,4,128,768]{3,2,1,0:T(8,128)(2,1)S(1)} copy(bf16[4,4,128,768]{3,2,0,1:T(8,128)(2,1)} %bitcast.15) | data formatting | bytes 6291456 | tf_op jit(solution)/shard_map/transpose | solution.py:63
  100.3 9.4 %gather_fusion = bf16[2048,768]{1,0:T(8,128)(2,1)} fusion(bf16[2048,768]{1,0:T(8,128)(2,1)S(1)} %bitcast.13, s32[2048]{0:T(1024)S(1)} %fusion.10), kind=kCustom, calls=%fused_computation | custom fusion | bytes 6299648 | tf_op jit(solution)/shard_map/jit(_take)/gather | solution.py:67
  109.7 4.3 %multiply_reduce_fusion = (f32[2048]{0:T(1024)S(1)}, bf16[2048,768]{1,0:T(8,128)(2,1)S(1)}, f32[2048]{0:T(1024)S(1)}) fusion(bf16[2048,768]{1,0:T(8,128)(2,1)} %gather_fusion, pred[2048]{0:T(1024)(128)(4,1)S(1)} %compare_and_fusion, bf16[2048,768]{1,0:T(8,128)(2,1)} %param.5), kind=kLoop, calls=%fused_computation.5 | loop fusion | flops 15724544 | bytes 9455616 | tf_op jit(solution)/shard_map/reduce_sum | solution.py:18
  114.0 1.7 copy-done.1
  115.7 3.3 %fusion.2 = f32[512,768]{1,0:T(8,128)} fusion(bf16[2048,768]{1,0:T(8,128)(2,1)S(1)} %get-tuple-element.11, s32[512]{0:T(512)S(1)} %iota_add_fusion, s32[2048]{0:T(1024)S(1)} %copy-done.4), kind=kOutput, calls=%fused_computation.7 | convolution fusion | flops 1611661312 | bytes 4728832 | tf_op jit(solution)/shard_map/dot_general | solution.py:34
  119.0 1.4 multiply_reduce_fusion.2
  120.4 1.4 multiply_reduce_fusion.1
  121.8 4.3 %add_reduce_fusion = f32[2048]{0:T(1024)S(1)} fusion(bf16[2048,768]{1,0:T(8,128)(2,1)} %copy-done.1, bf16[512,768]{1,0:T(8,128)(2,1)} %param.9, f32[512]{0:T(512)S(1)} %multiply_reduce_fusion.1, f32[2048]{0:T(1024)S(1)} %get-tuple-element.10), kind=kOutput, calls=%fused_computation.12 | convolution fusion | flops 1614804992 | bytes 3950592 | tf_op jit(solution)/shard_map/dot_general | solution.py:20
  126.2 1.8 add_reduce_fusion.1
  128.0 11.0 %all-reduce.3 = (f32[2048]{0:T(1024)S(1)}, f32[2048]{0:T(1024)S(1)}) all-reduce(f32[2048]{0:T(1024)S(1)} %add_reduce_fusion, f32[2048]{0:T(1024)S(1)} %add_reduce_fusion.1), channel_id=1, replica_groups=mesh['groups'=2,'pts'=4,'cb'=4] {'cb'}, use_global_device_ids=true, to_apply=%region_15.16 | all-reduce | flops 4096 | bytes 32768 | tf_op jit(solution)/shard_map/pmin | solution.py:25
  140.2 11.1 %all-reduce.2 = (f32[512]{0:T(512)S(1)}, f32[1]{0:T(128)}, f32[1]{0:T(128)}) all-reduce(f32[512]{0:T(512)S(1)} %get-tuple-element.3, f32[1]{0:T(128)} %bitcast.4, f32[1]{0:T(128)} %bitcast.3), channel_id=5, replica_groups=mesh['groups'=2,'pts'=4,'cb'=4] {'pts'}, use_global_device_ids=true, to_apply=%region_5.0.clone | all-reduce | flops 514 | bytes 4112
  151.4 1.9 %reduce-scatter.5.cloned.1.call-done = f32[128,768]{1,0:T(8,128)} async-done(((f32[512,768]{1,0:T(8,128)}), f32[128,768]{1,0:T(8,128)}) %reduce-scatter.5.cloned.1.call-update) | async-done | bytes 393232 | tf_op jit(solution)/shard_map/reduce_scatter | solution.py:39
  153.3 1.1 divide_convert_fusion
  154.6 7.9 %collective-permute-done = bf16[128,768]{1,0:T(8,128)(2,1)S(1)} collective-permute-done((bf16[128,768]{1,0:T(8,128)(2,1)S(1)}, bf16[128,768]{1,0:T(8,128)(2,1)S(1)}, u32[]{:S(2)}, u32[]{:S(2)}) %collective-permute-start) | collective-permute-done | bytes 196640 | tf_op jit(solution)/shard_map/ppermute | solution.py:11
  162.5 7.6 %collective-permute-done.1 = bf16[128,768]{1,0:T(8,128)(2,1)} collective-permute-done((bf16[128,768]{1,0:T(8,128)(2,1)S(1)}, bf16[128,768]{1,0:T(8,128)(2,1)}, u32[]{:S(2)}, u32[]{:S(2)}) %collective-permute-start.1) | collective-permute-done | bytes 196640 | tf_op jit(solution)/shard_map/ppermute | solution.py:11
  170.1 1.9 %maximum_multiply_fusion = f32[2]{0:T(128)} fusion(f32[1]{0:T(128)} %get-tuple-element.6, f32[1]{0:T(128)} %get-tuple-element.7), kind=kLoop, calls=%fused_computation.38 | loop fusion | flops 4 | bytes 16 | tf_op jit(solution)/shard_map/div | solution.py:75
  172.9 4.9 %collective-permute-done.2 = bf16[128,768]{1,0:T(8,128)(2,1)S(1)} collective-permute-done((bf16[128,768]{1,0:T(8,128)(2,1)}, bf16[128,768]{1,0:T(8,128)(2,1)S(1)}, u32[]{:S(2)}, u32[]{:S(2)}) %collective-permute-start.2) | collective-permute-done | bytes 196640 | tf_op jit(solution)/shard_map/ppermute | solution.py:11
  177.8 0.9 constant_dynamic-update-slice_fusion.6
  (37 shorter events, 5.3 us)
Async XLA Ops:
  7.2 43.7 %reduce-scatter.3.cloned.1.call-start = ((), (), s32[]{:S(2)}) async-start(), calls=%async_computation.2 | async-start | bytes 1966080 | tf_op jit(solution)/shard_map/reduce_scatter | solution.py:39
  7.2 5.3 %copy-start.5 = (u32[32]{0:T(128)S(1)}, u32[32]{0:T(128)}, u32[]{:S(2)}) copy-start(u32[32]{0:T(128)} %constant.64) | copy-start | bytes 388
  7.2 6.6 %copy-start.3 = (s32[2048]{0:T(1024)S(1)}, s32[2048]{0:T(1024)}, u32[]{:S(2)}) copy-start(s32[2048]{0:T(1024)} %param.6) | copy-start | bytes 24580
  7.3 6.6 %copy-start.4 = (s32[2048]{0:T(1024)S(1)}, s32[2048]{0:T(1024)}, u32[]{:S(2)}) copy-start(s32[2048]{0:T(1024)} %param.7) | copy-start | bytes 24580
  12.5 85.7 %all-gather.2.cloned.1.call-start = ((), (), s32[]{:S(2)}) async-start(), calls=%async_computation.3 | async-start | bytes 3342336 | tf_op jit(solution)/shard_map/all_gather | solution.py:61
  52.8 100.5 %reduce-scatter.5.cloned.1.call-start = ((), (), s32[]{:S(2)}) async-start(), calls=%async_computation.4 | async-start | bytes 1966080 | tf_op jit(solution)/shard_map/reduce_scatter | solution.py:39
  114.0 1.7 copy-start.1
  121.8 4.4 %copy-start = (bf16[2048,768]{1,0:T(8,128)(2,1)S(1)}, bf16[2048,768]{1,0:T(8,128)(2,1)}, u32[]{:S(2)}) copy-start(bf16[2048,768]{1,0:T(8,128)(2,1)} %param.5) | copy-start | bytes 9437188
  121.8 4.4 %copy-start.2 = (bf16[512,768]{1,0:T(8,128)(2,1)S(1)}, bf16[512,768]{1,0:T(8,128)(2,1)}, u32[]{:S(2)}) copy-start(bf16[512,768]{1,0:T(8,128)(2,1)} %param.8) | copy-start | bytes 2359300
  154.4 8.1 %collective-permute-start = (bf16[128,768]{1,0:T(8,128)(2,1)S(1)}, bf16[128,768]{1,0:T(8,128)(2,1)S(1)}, u32[]{:S(2)}, u32[]{:S(2)}) collective-permute-start(bf16[128,768]{1,0:T(8,128)(2,1)S(1)} %divide_convert_fusion), channel_id=1, source_target_pairs={{0,4},{4,8},{8,12},{12,0},{1,5},{5,9},{9,13},{13,1},{2,6},{6,10},{... | collective-permute-start | bytes 589832 | tf_op jit(solution)/shard_map/ppermute | solution.py:11
  162.5 7.6 %collective-permute-start.1 = (bf16[128,768]{1,0:T(8,128)(2,1)S(1)}, bf16[128,768]{1,0:T(8,128)(2,1)}, u32[]{:S(2)}, u32[]{:S(2)}) collective-permute-start(bf16[128,768]{1,0:T(8,128)(2,1)S(1)} %collective-permute-done), channel_id=1, source_target_pairs={{0,4},{4,8},{8,12},{12,0},{1,5},{5,9},{9,13},{13,1},{2,6},{6,10},{... | collective-permute-start | bytes 589832 | tf_op jit(solution)/shard_map/ppermute | solution.py:11
  170.1 7.7 %collective-permute-start.2 = (bf16[128,768]{1,0:T(8,128)(2,1)}, bf16[128,768]{1,0:T(8,128)(2,1)S(1)}, u32[]{:S(2)}, u32[]{:S(2)}) collective-permute-start(bf16[128,768]{1,0:T(8,128)(2,1)} %collective-permute-done.1), channel_id=1, source_target_pairs={{0,4},{4,8},{8,12},{12,0},{1,5},{5,9},{9,13},{13,1},{2,6},{6,10},{... | collective-permute-start | bytes 589832 | tf_op jit(solution)/shard_map/ppermute | solution.py:11
Sparse Core Ops, SparseCore 0:
  12.6 38.2 reduce-scatter.2
  53.8 44.3 all-gather.1
  119.2 34.0 reduce-scatter.4
